TPU v7x, 32 devices: a whole 2x2x4 slice. The times are simulated.
32 devices in a mesh: row: 4 (over y, core), col: 8 (over z, x).
Axes of the slice: x: 2, y: 2, z: 4, core: 2. Of those that a mesh axis runs over, the one named last changes fastest.
Arguments:
- matrix: float32 [16384, 16384], P('row', 'col'), may hold values from -500 to 500
Outputs:
- reduced: float32 [16384, 16384], P('row', 'col')
All inputs are finite; a program needn't handle non-finite values.
Results may differ from a plain program's by a relative error of at most 0.0003.
Values sent between devices are 32-bit elements; how exact they have to be, the bound alone decides.
A program may use at most 192 MiB of HBM per device.

v0:
```python
import jax
import jax.numpy as jnp
from jax import lax
from jax.sharding import PartitionSpec as P

REFL = 4
PANELS = 2
highest = lax.Precision.HIGHEST


def from_root(value, axis, source):
    kept = jnp.where(lax.axis_index(axis) == source, value, 0).astype(value.dtype)
    return lax.psum(kept, axis)


def product(left, right):
    return jnp.dot(left, right, precision=highest, preferred_element_type=jnp.float32)


def on_device(matrix):
    rows_local, cols_local = matrix.shape
    row_start = lax.axis_index("row") * rows_local
    col_start = lax.axis_index("col") * cols_local
    total = rows_local * lax.axis_size("row")
    positions = jnp.arange(total, dtype=jnp.int32)
    current = matrix
    for panel_index in range(PANELS):
        reflectors = jnp.zeros((total, REFL), jnp.float32)
        updates = jnp.zeros((total, REFL), jnp.float32)
        for inner_index in range(REFL):
            target = panel_index * REFL + inner_index
            owner = target // cols_local
            own_slice = current[:, target - owner * cols_local]
            reflector_rows = lax.dynamic_slice_in_dim(reflectors, row_start, rows_local, 0)
            update_block = lax.dynamic_slice_in_dim(updates, row_start, rows_local, 0)
            held = from_root(own_slice, "col", owner)
            column = (
                held
                - product(reflector_rows, updates[target])
                - product(update_block, reflectors[target])
            )
            whole = lax.all_gather(column, "row", axis=0, tiled=True)
            beneath = jnp.where(positions > target, whole, 0.0)
            leading = whole[target + 1]
            length = jnp.sqrt(jnp.sum(beneath * beneath))
            signed = jnp.where(leading >= 0.0, length, -length)
            vector = beneath + jnp.where(positions == target + 1, signed, 0.0)
            factor = 1.0 / (length * (length + jnp.abs(leading)))
            vector_cols = lax.dynamic_slice_in_dim(vector, col_start, cols_local, 0)
            against_updates = product(vector, updates)
            against_reflectors = product(vector, reflectors)
            summed = lax.psum(product(current, vector_cols), "col")
            mapped = factor * (
                summed
                - product(reflector_rows, against_updates)
                - product(update_block, against_reflectors)
            )
            vector_rows = lax.dynamic_slice_in_dim(vector, row_start, rows_local, 0)
            inner = lax.psum(jnp.sum(mapped * vector_rows), "row")
            update = lax.all_gather(
                mapped - 0.5 * factor * inner * vector_rows, "row", axis=0, tiled=True
            )
            reflectors = reflectors.at[:, inner_index].set(vector)
            updates = updates.at[:, inner_index].set(update)
        reflector_rows = lax.dynamic_slice_in_dim(reflectors, row_start, rows_local, 0)
        update_block = lax.dynamic_slice_in_dim(updates, row_start, rows_local, 0)
        reflector_cols = lax.dynamic_slice_in_dim(reflectors, col_start, cols_local, 0)
        update_cols = lax.dynamic_slice_in_dim(updates, col_start, cols_local, 0)
        current = (
            current
            - product(reflector_rows, update_cols.T)
            - product(update_block, reflector_cols.T)
        )
    return current


def solution(mesh):
    return jax.shard_map(
        on_device,
        mesh=mesh,
        in_specs=(P("row", "col"),),
        out_specs=P("row", "col"),
        check_vma=False,
    )
```

profile of v0, /device:TPU:0, one launch (start us, length us, event | category | flops | bytes accessed | tf_op | source)
XLA Modules:
  0.0 982.2 jit_solution(17959320532915637002)
XLA Ops:
  3.4 31.1 %copy.46 = f32[4096,2048]{0,1:T(8,128)} copy(f32[4096,2048]{1,0:T(8,128)} %param.33) | data formatting | bytes 67108864 | tf_op args[0]
  35.8 38.8 %psum.168 = f32[4096]{0:T(1024)S(1)} all-reduce(f32[4096]{0:T(1024)S(1)} %bitcast.324), channel_id=1, replica_groups=mesh['row'=4,'col'=8] {'col'}, use_global_device_ids=true, to_apply=%region_1.2 | all-reduce | flops 4096 | bytes 32768 | tf_op jit(solution)/shard_map/psum | solution.py:13
  74.7 5.2 all_gather.48
  85.9 30.7 %fusion.128 = f32[1,4096]{1,0:T(1,128)S(1)} fusion(f32[2048,1]{0,1:T(1,128)S(1)} %bitcast.325, f32[4096,2048]{1,0:T(8,128)} %param.33), kind=kOutput, calls=%fused_computation.249 | convolution fusion | flops 100663296 | bytes 33579008 | tf_op jit(solution)/shard_map/dot_general | solution.py:17
  116.6 33.1 %all-reduce.9 = (f32[4096]{0:T(1024)S(1)}, f32[4096]{0:T(1024)S(1)}) all-reduce(f32[4096]{0:T(1024)S(1)} %bitcast.289, f32[4096]{0:T(1024)S(1)} %bitcast.322), channel_id=1, replica_groups=mesh['row'=4,'col'=8] {'col'}, use_global_device_ids=true, to_apply=%region_5.6 | all-reduce | flops 8192 | bytes 65536 | tf_op jit(solution)/shard_map/psum | solution.py:52
  151.1 6.3 psum.171
  158.1 5.2 all_gather.49
  164.8 5.5 all_gather.50
  176.8 30.7 %fusion.129 = f32[1,4096]{1,0:T(1,128)S(1)} fusion(f32[2048,1]{0,1:T(1,128)S(1)} %bitcast.326, f32[4096,2048]{1,0:T(8,128)} %param.33), kind=kOutput, calls=%fused_computation.250 | convolution fusion | flops 100663296 | bytes 33579008 | tf_op jit(solution)/shard_map/dot_general | solution.py:17
  207.5 33.1 %all-reduce.8 = (f32[4096]{0:T(1024)S(1)}, f32[4096]{0:T(1024)S(1)}) all-reduce(f32[4096]{0:T(1024)S(1)} %bitcast.290, f32[4096]{0:T(1024)S(1)} %bitcast.320), channel_id=1, replica_groups=mesh['row'=4,'col'=8] {'col'}, use_global_device_ids=true, to_apply=%region_11.12 | all-reduce | flops 8192 | bytes 65536 | tf_op jit(solution)/shard_map/psum | solution.py:52
  241.8 6.3 psum.174
  248.6 5.2 all_gather.51
  257.9 5.7 all_gather.52
  269.5 30.7 %fusion.130 = f32[1,4096]{1,0:T(1,128)S(1)} fusion(f32[2048,1]{0,1:T(1,128)S(1)} %bitcast.327, f32[4096,2048]{1,0:T(8,128)} %param.33), kind=kOutput, calls=%fused_computation.251 | convolution fusion | flops 100663296 | bytes 33579008 | tf_op jit(solution)/shard_map/dot_general | solution.py:17
  300.2 33.1 %all-reduce.7 = (f32[4096]{0:T(1024)S(1)}, f32[4096]{0:T(1024)S(1)}) all-reduce(f32[4096]{0:T(1024)S(1)} %bitcast.291, f32[4096]{0:T(1024)S(1)} %bitcast.318), channel_id=1, replica_groups=mesh['row'=4,'col'=8] {'col'}, use_global_device_ids=true, to_apply=%region_16.17 | all-reduce | flops 8192 | bytes 65536 | tf_op jit(solution)/shard_map/psum | solution.py:52
  334.5 6.3 psum.177
  341.3 5.2 all_gather.53
  351.4 5.5 all_gather.54
  362.8 30.7 %fusion.131 = f32[1,4096]{1,0:T(1,128)S(1)} fusion(f32[2048,1]{0,1:T(1,128)S(1)} %bitcast.328, f32[4096,2048]{1,0:T(8,128)} %param.33), kind=kOutput, calls=%fused_computation.252 | convolution fusion | flops 100663296 | bytes 33579008 | tf_op jit(solution)/shard_map/dot_general | solution.py:17
  393.5 33.0 %psum.178 = f32[4096]{0:T(1024)S(1)} all-reduce(f32[4096]{0:T(1024)S(1)} %bitcast.292), channel_id=1, replica_groups=mesh['row'=4,'col'=8] {'col'}, use_global_device_ids=true, to_apply=%region_20.21 | all-reduce | flops 4096 | bytes 32768 | tf_op jit(solution)/shard_map/psum | solution.py:52
  428.9 6.3 psum.179
  435.7 5.4 all_gather.55
  442.3 30.1 %fusion.14 = f32[4096,2048]{0,1:T(8,128)} fusion(f32[16384,4]{0,1:T(4,128)S(1)} %scatter.64, s32[]{:T(128)S(6)} %select_n.183, f32[16384,4]{0,1:T(4,128)S(1)} %scatter.65, s32[]{:T(128)S(6)} %select_n.184), kind=kOutput, calls=%fused_computation.58 | convolution fusion | flops 402653184 | bytes 33652744 | tf_op jit(solution)/shard_map/dot_general | solution.py:17
  472.4 41.2 %subtract_subtract_fusion.1 = f32[4096,2048]{0,1:T(8,128)} fusion(f32[4096,2048]{0,1:T(8,128)} %copy.46, f32[4096,2048]{0,1:T(8,128)} %fusion.14, f32[16384,4]{0,1:T(4,128)S(1)} %scatter.65, s32[]{:T(128)S(6)} %select_n.183, f32[16384,4]{0,1:T(4,128)S(1)} %scatter.64, s32[]{:T(128)S(6)} %select_n.184), kind=kOutput, calls=%fused_computation.1 | convolution fusion | flops 419430400 | bytes 100761608 | tf_op jit(solution)/shard_map/dot_general | solution.py:17
  515.0 33.0 %psum.180 = f32[4096]{0:T(1024)S(1)} all-reduce(f32[4096]{0:T(1024)S(1)} %bitcast.323), channel_id=1, replica_groups=mesh['row'=4,'col'=8] {'col'}, use_global_device_ids=true, to_apply=%region_23.24 | all-reduce | flops 4096 | bytes 32768 | tf_op jit(solution)/shard_map/psum | solution.py:13
  548.0 5.2 all_gather.56
  559.2 21.5 %fusion.132 = f32[1,4096]{1,0:T(1,128)S(1)} fusion(f32[4096,2048]{0,1:T(8,128)} %subtract_subtract_fusion.1, f32[2048,1]{0,1:T(1,128)S(1)} %bitcast.329), kind=kOutput, calls=%fused_computation.253 | convolution fusion | flops 100663296 | bytes 33579008 | tf_op jit(solution)/shard_map/dot_general | solution.py:17
  580.7 33.1 %all-reduce.6 = (f32[4096]{0:T(1024)S(1)}, f32[4096]{0:T(1024)S(1)}) all-reduce(f32[4096]{0:T(1024)S(1)} %bitcast.285, f32[4096]{0:T(1024)S(1)} %bitcast.321), channel_id=1, replica_groups=mesh['row'=4,'col'=8] {'col'}, use_global_device_ids=true, to_apply=%region_26.27 | all-reduce | flops 8192 | bytes 65536 | tf_op jit(solution)/shard_map/psum | solution.py:52
  615.2 6.3 psum.183
  622.2 5.2 all_gather.57
  628.9 5.4 all_gather.58
  640.8 21.0 %fusion.133 = f32[1,4096]{1,0:T(1,128)S(1)} fusion(f32[4096,2048]{0,1:T(8,128)} %subtract_subtract_fusion.1, f32[2048,1]{0,1:T(1,128)S(1)} %bitcast.330), kind=kOutput, calls=%fused_computation.254 | convolution fusion | flops 100663296 | bytes 33579008 | tf_op jit(solution)/shard_map/dot_general | solution.py:17
  661.9 33.2 %all-reduce.5 = (f32[4096]{0:T(1024)S(1)}, f32[4096]{0:T(1024)S(1)}) all-reduce(f32[4096]{0:T(1024)S(1)} %bitcast.286, f32[4096]{0:T(1024)S(1)} %bitcast.319), channel_id=1, replica_groups=mesh['row'=4,'col'=8] {'col'}, use_global_device_ids=true, to_apply=%region_31.32 | all-reduce | flops 8192 | bytes 65536 | tf_op jit(solution)/shard_map/psum | solution.py:52
  696.3 6.3 psum.186
  703.2 5.2 all_gather.59
  712.4 5.3 all_gather.60
  723.6 21.0 %fusion.134 = f32[1,4096]{1,0:T(1,128)S(1)} fusion(f32[4096,2048]{0,1:T(8,128)} %subtract_subtract_fusion.1, f32[2048,1]{0,1:T(1,128)S(1)} %bitcast.331), kind=kOutput, calls=%fused_computation.255 | convolution fusion | flops 100663296 | bytes 33579008 | tf_op jit(solution)/shard_map/dot_general | solution.py:17
  744.7 33.1 %all-reduce.4 = (f32[4096]{0:T(1024)S(1)}, f32[4096]{0:T(1024)S(1)}) all-reduce(f32[4096]{0:T(1024)S(1)} %bitcast.287, f32[4096]{0:T(1024)S(1)} %bitcast.317), channel_id=1, replica_groups=mesh['row'=4,'col'=8] {'col'}, use_global_device_ids=true, to_apply=%region_36.37 | all-reduce | flops 8192 | bytes 65536 | tf_op jit(solution)/shard_map/psum | solution.py:52
  778.9 6.3 psum.189
  785.8 5.2 all_gather.61
  795.9 5.6 all_gather.62
  807.3 21.0 %fusion.135 = f32[1,4096]{1,0:T(1,128)S(1)} fusion(f32[4096,2048]{0,1:T(8,128)} %subtract_subtract_fusion.1, f32[2048,1]{0,1:T(1,128)S(1)} %bitcast.332), kind=kOutput, calls=%fused_computation.256 | convolution fusion | flops 100663296 | bytes 33579008 | tf_op jit(solution)/shard_map/dot_general | solution.py:17
  828.3 33.0 %psum.190 = f32[4096]{0:T(1024)S(1)} all-reduce(f32[4096]{0:T(1024)S(1)} %bitcast.288), channel_id=1, replica_groups=mesh['row'=4,'col'=8] {'col'}, use_global_device_ids=true, to_apply=%region_40.41 | all-reduce | flops 4096 | bytes 32768 | tf_op jit(solution)/shard_map/psum | solution.py:52
  863.7 6.3 psum.191
  870.6 5.5 all_gather.63
  877.2 30.1 %fusion.11 = f32[4096,2048]{0,1:T(8,128)} fusion(f32[16384,4]{0,1:T(4,128)S(1)} %scatter.76, s32[]{:T(128)S(6)} %select_n.183, f32[16384,4]{0,1:T(4,128)S(1)} %scatter.79, s32[]{:T(128)S(6)} %select_n.184), kind=kOutput, calls=%fused_computation.39 | convolution fusion | flops 402653184 | bytes 33652744 | tf_op jit(solution)/shard_map/dot_general | solution.py:17
  907.3 41.1 %subtract_subtract_fusion = f32[4096,2048]{0,1:T(8,128)} fusion(f32[4096,2048]{0,1:T(8,128)} %subtract_subtract_fusion.1, f32[4096,2048]{0,1:T(8,128)} %fusion.11, f32[16384,4]{0,1:T(4,128)S(1)} %scatter.79, s32[]{:T(128)S(6)} %select_n.183, f32[16384,4]{0,1:T(4,128)S(1)} %scatter.76, s32[]{:T(128)S(6)} %select_n.184), kind=kOutput, calls=%fused_computation | convolution fusion | flops 419430400 | bytes 100761608 | tf_op jit(solution)/shard_map/dot_general | solution.py:17
  948.4 33.3 %copy.49 = f32[4096,2048]{1,0:T(8,128)} copy(f32[4096,2048]{0,1:T(8,128)} %subtract_subtract_fusion) | data formatting | bytes 67108864 | tf_op jit(solution)/shard_map/sub | solution.py:70
  (139 shorter events, 73.5 us)
where the time goes:
time: 991 us; the launch traced here: 982 us
  blocking collectives  472 us (48%)
  matrix products  376 us (38%)
  local copies, waits for them, and re-layouts  87.7 us (9%)
  other arithmetic  24.6 us (2%)
  between operations  22 us (2%)
    dot_general x50, matrix products, product(): jnp.dot(left, right, precision=highest, preferred_element_type=jnp.float32)  376 us
    psum x8, blocking collectives, on_device(): summed = lax.psum(product(current, vector_cols), 'col')  264 us
    psum x2, blocking collectives, from_root(): return lax.psum(kept, axis)  71.8 us
    psum x8, blocking collectives, on_device(): inner = lax.psum(jnp.sum(mapped * vector_rows), 'row')  50.2 us
    all_gather x8, blocking collectives, on_device(): whole = lax.all_gather(column, 'row', axis=0, tiled=True)  43.5 us
    all_gather x8, blocking collectives, on_device(): lax.all_gather(mapped - 0.5 * factor * inner * vector_rows, 'row', axis=0...  42.4 us
    sub x1, local copies, waits for them, and re-layouts, on_device(): current - product(reflector_rows, update_cols.T)  33.3 us
    unnamed x1, local copies, waits for them, and re-layouts  31.1 us

commit v1 on v0

--- a/solution.py
+++ b/solution.py
@@ -6,6 +6,10 @@
 REFL = 4
 PANELS = 2
 highest = lax.Precision.HIGHEST
+
+
+def plan_the_pieces_all(local_block):
+    return lax.all_gather(local_block, "col").sum(axis=0)
 
 
 def from_root(value, axis, source):
@@ -49,7 +53,7 @@
             vector_cols = lax.dynamic_slice_in_dim(vector, col_start, cols_local, 0)
             against_updates = product(vector, updates)
             against_reflectors = product(vector, reflectors)
-            summed = lax.psum(product(current, vector_cols), "col")
+            summed = plan_the_pieces_all(product(current, vector_cols))
             mapped = factor * (
                 summed
                 - product(reflector_rows, against_updates)

time: 991 us -> 1060 us (1.070)
  waiting for transfers between devices: 0 us -> 141 us
  blocking collectives: 472 us -> 380 us
  between operations: 22 us -> 35.3 us
    psum x10 -> x0, blocking collectives: 336 us -> none  [the longest x8 264 us: on_device(): summed = lax.psum(product(current, vector_cols), 'col')]
    all_gather x0 -> x8, blocking collectives: none -> 244 us  [plan_the_pieces_all(): return lax.all_gather(local_block, 'col').sum(axis=0)]
    psum x0 -> x2, waiting for transfers between devices: none -> 141 us  [from_root(): return lax.psum(kept, axis)]
    unnamed x1 -> x13, local copies, waits for them, and re-layouts: 31.1 us -> 31.1 us
  transfers between devices with their start and end apart: 0 -> 2, of which waited for: 0 -> 2; matrix products, arithmetic and copies ran while one was open for 0% -> 0% of each run, Pallas kernels for 0% -> 0%
where the time goes in v1:
time: 1060 us; the launch traced here: 1050 us
  blocking collectives  380 us (36%)
  matrix products  376 us (35%)
  waiting for transfers between devices  141 us (13%)
  local copies, waits for them, and re-layouts  88.1 us (8%)
  between operations  35.3 us (3%)
  other arithmetic  27.3 us (3%)
    dot_general x50, matrix products, product(): jnp.dot(left, right, precision=highest, preferred_element_type=jnp.float32)  376 us
    all_gather x8, blocking collectives, plan_the_pieces_all(): return lax.all_gather(local_block, 'col').sum(axis=0)  244 us
    psum x2, waiting for transfers between devices, from_root(): return lax.psum(kept, axis)  141 us
    psum x8, blocking collectives, on_device(): inner = lax.psum(jnp.sum(mapped * vector_rows), 'row')  50.4 us
    all_gather x8, blocking collectives, on_device(): whole = lax.all_gather(column, 'row', axis=0, tiled=True)  43.2 us
    all_gather x8, blocking collectives, on_device(): lax.all_gather(mapped - 0.5 * factor * inner * vector_rows, 'row', axis=0...  42.1 us
    sub x1, local copies, waits for them, and re-layouts, on_device(): current - product(reflector_rows, update_cols.T)  33.3 us
    unnamed x13, local copies, waits for them, and re-layouts  31.1 us
  transfers between devices with their start and end apart: 2, of which 2 were waited for; matrix products, arithmetic and copies ran while one was open for 0% of the time, Pallas kernels for 0%

profile of v1, /device:TPU:0, one launch (start us, length us, event | category | flops | bytes accessed | tf_op | source)
XLA Modules:
  0.0 1047.9 jit_solution(17656806992550677127)
XLA Ops:
  6.5 31.1 %copy.46 = f32[4096,2048]{0,1:T(8,128)} copy(f32[4096,2048]{1,0:T(8,128)} %param.33) | data formatting | bytes 67108864 | tf_op args[0]
  42.4 70.3 %all-reduce.11.cloned.1.call-done = (f32[4096]{0:T(1024)}, f32[4096]{0:T(1024)}, f32[4096]{0:T(1024)}, f32[4096]{0:T(1024)}) async-done(((f32[4096]{0:T(1024)}, f32[4096]{0:T(1024)}, f32[4096]{0:T(1024)}, f32[4096]{0:T(1024)}), (f32[4096]{0:T(1024)}, f32[4096]{0:T(1024)}, f32[4096]{0:T(1024)}, f32[4096]{0:T(1024)})) %all-reduce.11.cloned.1.call-update) | async-done | bytes 65552 | tf_op jit(solution)/shard_map/psum | solution.py:17
  113.9 5.2 all_gather.96
  125.2 30.7 %fusion.128 = f32[1,4096]{1,0:T(1,128)S(1)} fusion(f32[2048,1]{0,1:T(1,128)S(1)} %bitcast.328, f32[4096,2048]{1,0:T(8,128)} %param.33), kind=kOutput, calls=%fused_computation.249 | convolution fusion | flops 100663296 | bytes 33579008 | tf_op jit(solution)/shard_map/dot_general | solution.py:21
  155.9 30.6 %all-gather = f32[32768]{0:T(1024)S(1)} all-gather(f32[4096]{0:T(1024)S(1)} %bitcast.292), channel_id=2, replica_groups=mesh['row'=4,'col'=8] {'col'}, dimensions={0}, use_global_device_ids=true | all-gather | bytes 147456 | tf_op jit(solution)/shard_map/all_gather | solution.py:12
  187.9 6.3 psum.114
  194.9 5.2 all_gather.99
  201.6 5.7 all_gather.100
  213.9 30.7 %fusion.129 = f32[1,4096]{1,0:T(1,128)S(1)} fusion(f32[2048,1]{0,1:T(1,128)S(1)} %bitcast.325, f32[4096,2048]{1,0:T(8,128)} %param.33), kind=kOutput, calls=%fused_computation.250 | convolution fusion | flops 100663296 | bytes 33579008 | tf_op jit(solution)/shard_map/dot_general | solution.py:21
  245.1 30.5 %all-gather.1 = f32[32768]{0:T(1024)S(1)} all-gather(f32[4096]{0:T(1024)S(1)} %bitcast.290), channel_id=3, replica_groups=mesh['row'=4,'col'=8] {'col'}, dimensions={0}, use_global_device_ids=true | all-gather | bytes 147456 | tf_op jit(solution)/shard_map/all_gather | solution.py:12
  276.3 6.3 psum.116
  283.3 5.2 all_gather.103
  292.4 5.5 all_gather.104
  303.9 30.7 %fusion.130 = f32[1,4096]{1,0:T(1,128)S(1)} fusion(f32[2048,1]{0,1:T(1,128)S(1)} %bitcast.326, f32[4096,2048]{1,0:T(8,128)} %param.33), kind=kOutput, calls=%fused_computation.251 | convolution fusion | flops 100663296 | bytes 33579008 | tf_op jit(solution)/shard_map/dot_general | solution.py:21
  337.3 30.5 %all-gather.2 = f32[32768]{0:T(1024)S(1)} all-gather(f32[4096]{0:T(1024)S(1)} %bitcast.289), channel_id=4, replica_groups=mesh['row'=4,'col'=8] {'col'}, dimensions={0}, use_global_device_ids=true | all-gather | bytes 147456 | tf_op jit(solution)/shard_map/all_gather | solution.py:12
  368.5 6.3 psum.118
  375.5 5.2 all_gather.107
  383.4 5.5 all_gather.108
  394.9 30.7 %fusion.131 = f32[1,4096]{1,0:T(1,128)S(1)} fusion(f32[2048,1]{0,1:T(1,128)S(1)} %bitcast.327, f32[4096,2048]{1,0:T(8,128)} %param.33), kind=kOutput, calls=%fused_computation.252 | convolution fusion | flops 100663296 | bytes 33579008 | tf_op jit(solution)/shard_map/dot_general | solution.py:21
  426.1 30.5 %all-gather.3 = f32[32768]{0:T(1024)S(1)} all-gather(f32[4096]{0:T(1024)S(1)} %bitcast.291), channel_id=5, replica_groups=mesh['row'=4,'col'=8] {'col'}, dimensions={0}, use_global_device_ids=true | all-gather | bytes 147456 | tf_op jit(solution)/shard_map/all_gather | solution.py:12
  458.6 6.3 psum.119
  465.4 5.5 all_gather.111
  472.1 30.1 %fusion.14 = f32[4096,2048]{0,1:T(8,128)} fusion(f32[16384,4]{0,1:T(4,128)S(1)} %scatter.64, s32[]{:T(128)S(6)} %select_n.183, f32[16384,4]{0,1:T(4,128)S(1)} %scatter.65, s32[]{:T(128)S(6)} %select_n.184), kind=kOutput, calls=%fused_computation.58 | convolution fusion | flops 402653184 | bytes 33652744 | tf_op jit(solution)/shard_map/dot_general | solution.py:21
  502.2 41.5 %subtract_subtract_fusion.1 = f32[4096,2048]{0,1:T(8,128)} fusion(f32[4096,2048]{0,1:T(8,128)} %copy.46, f32[4096,2048]{0,1:T(8,128)} %fusion.14, f32[16384,4]{0,1:T(4,128)S(1)} %scatter.65, s32[]{:T(128)S(6)} %select_n.183, f32[16384,4]{0,1:T(4,128)S(1)} %scatter.64, s32[]{:T(128)S(6)} %select_n.184), kind=kOutput, calls=%fused_computation.1 | convolution fusion | flops 419430400 | bytes 100761608 | tf_op jit(solution)/shard_map/dot_general | solution.py:21
  545.6 70.5 %all-reduce.9.cloned.1.call-done = (f32[4096]{0:T(1024)}, f32[4096]{0:T(1024)}, f32[4096]{0:T(1024)}, f32[4096]{0:T(1024)}) async-done(((f32[4096]{0:T(1024)}, f32[4096]{0:T(1024)}, f32[4096]{0:T(1024)}, f32[4096]{0:T(1024)}), (f32[4096]{0:T(1024)}, f32[4096]{0:T(1024)}, f32[4096]{0:T(1024)}, f32[4096]{0:T(1024)})) %all-reduce.9.cloned.1.call-update) | async-done | bytes 65552 | tf_op jit(solution)/shard_map/psum | solution.py:17
  616.8 5.2 all_gather.112
  628.1 21.2 %fusion.132 = f32[1,4096]{1,0:T(1,128)S(1)} fusion(f32[4096,2048]{0,1:T(8,128)} %subtract_subtract_fusion.1, f32[2048,1]{0,1:T(1,128)S(1)} %bitcast.332), kind=kOutput, calls=%fused_computation.253 | convolution fusion | flops 100663296 | bytes 33579008 | tf_op jit(solution)/shard_map/dot_general | solution.py:21
  649.2 30.6 %all-gather.4 = f32[32768]{0:T(1024)S(1)} all-gather(f32[4096]{0:T(1024)S(1)} %bitcast.288), channel_id=6, replica_groups=mesh['row'=4,'col'=8] {'col'}, dimensions={0}, use_global_device_ids=true | all-gather | bytes 147456 | tf_op jit(solution)/shard_map/all_gather | solution.py:12
  681.3 6.3 psum.122
  688.2 5.2 all_gather.115
  694.9 5.3 all_gather.116
  706.7 21.2 %fusion.133 = f32[1,4096]{1,0:T(1,128)S(1)} fusion(f32[4096,2048]{0,1:T(8,128)} %subtract_subtract_fusion.1, f32[2048,1]{0,1:T(1,128)S(1)} %bitcast.329), kind=kOutput, calls=%fused_computation.254 | convolution fusion | flops 100663296 | bytes 33579008 | tf_op jit(solution)/shard_map/dot_general | solution.py:21
  728.5 30.5 %all-gather.5 = f32[32768]{0:T(1024)S(1)} all-gather(f32[4096]{0:T(1024)S(1)} %bitcast.286), channel_id=7, replica_groups=mesh['row'=4,'col'=8] {'col'}, dimensions={0}, use_global_device_ids=true | all-gather | bytes 147456 | tf_op jit(solution)/shard_map/all_gather | solution.py:12
  759.7 6.3 psum.124
  766.7 5.2 all_gather.119
  775.9 5.3 all_gather.120
  787.9 21.3 %fusion.134 = f32[1,4096]{1,0:T(1,128)S(1)} fusion(f32[4096,2048]{0,1:T(8,128)} %subtract_subtract_fusion.1, f32[2048,1]{0,1:T(1,128)S(1)} %bitcast.331), kind=kOutput, calls=%fused_computation.255 | convolution fusion | flops 100663296 | bytes 33579008 | tf_op jit(solution)/shard_map/dot_general | solution.py:21
  811.1 30.5 %all-gather.6 = f32[32768]{0:T(1024)S(1)} all-gather(f32[4096]{0:T(1024)S(1)} %bitcast.285), channel_id=8, replica_groups=mesh['row'=4,'col'=8] {'col'}, dimensions={0}, use_global_device_ids=true | all-gather | bytes 147456 | tf_op jit(solution)/shard_map/all_gather | solution.py:12
  842.3 6.3 psum.126
  849.3 5.2 all_gather.123
  857.2 5.3 all_gather.124
  868.5 21.5 %fusion.135 = f32[1,4096]{1,0:T(1,128)S(1)} fusion(f32[4096,2048]{0,1:T(8,128)} %subtract_subtract_fusion.1, f32[2048,1]{0,1:T(1,128)S(1)} %bitcast.330), kind=kOutput, calls=%fused_computation.256 | convolution fusion | flops 100663296 | bytes 33579008 | tf_op jit(solution)/shard_map/dot_general | solution.py:21
  891.7 30.5 %all-gather.7 = f32[32768]{0:T(1024)S(1)} all-gather(f32[4096]{0:T(1024)S(1)} %bitcast.287), channel_id=9, replica_groups=mesh['row'=4,'col'=8] {'col'}, dimensions={0}, use_global_device_ids=true | all-gather | bytes 147456 | tf_op jit(solution)/shard_map/all_gather | solution.py:12
  922.9 6.3 psum.127
  929.8 5.2 all_gather.127
  936.4 30.1 %fusion.11 = f32[4096,2048]{0,1:T(8,128)} fusion(f32[16384,4]{0,1:T(4,128)S(1)} %scatter.76, s32[]{:T(128)S(6)} %select_n.183, f32[16384,4]{0,1:T(4,128)S(1)} %scatter.79, s32[]{:T(128)S(6)} %select_n.184), kind=kOutput, calls=%fused_computation.39 | convolution fusion | flops 402653184 | bytes 33652744 | tf_op jit(solution)/shard_map/dot_general | solution.py:21
  966.5 41.0 %subtract_subtract_fusion = f32[4096,2048]{0,1:T(8,128)} fusion(f32[4096,2048]{0,1:T(8,128)} %subtract_subtract_fusion.1, f32[4096,2048]{0,1:T(8,128)} %fusion.11, f32[16384,4]{0,1:T(4,128)S(1)} %scatter.79, s32[]{:T(128)S(6)} %select_n.183, f32[16384,4]{0,1:T(4,128)S(1)} %scatter.76, s32[]{:T(128)S(6)} %select_n.184), kind=kOutput, calls=%fused_computation | convolution fusion | flops 419430400 | bytes 100761608 | tf_op jit(solution)/shard_map/dot_general | solution.py:21
  1007.5 33.3 %copy.49 = f32[4096,2048]{1,0:T(8,128)} copy(f32[4096,2048]{0,1:T(8,128)} %subtract_subtract_fusion) | data formatting | bytes 67108864 | tf_op jit(solution)/shard_map/sub | solution.py:74
  (171 shorter events, 76.7 us)
Async XLA Ops:
  6.5 106.1 %all-reduce.11.cloned.1.call-start = ((), (), s32[]{:S(2)}) async-start(), calls=%async_computation.1 | async-start | bytes 131072 | tf_op jit(solution)/shard_map/psum | solution.py:17
  39.5 576.6 %all-reduce.9.cloned.1.call-start = ((), (), s32[]{:S(2)}) async-start(), calls=%async_computation | async-start | bytes 131072 | tf_op jit(solution)/shard_map/psum | solution.py:17
  112.6 88.9 %copy-start.4 = (f32[4096]{0:T(1024)S(1)}, f32[4096]{0:T(1024)}, u32[]{:S(2)}) copy-start(f32[4096]{0:T(1024)} %get-tuple-element.202) | copy-start | bytes 49156
  125.1 167.3 %copy-start.2 = (f32[4096]{0:T(1024)S(1)}, f32[4096]{0:T(1024)}, u32[]{:S(2)}) copy-start(f32[4096]{0:T(1024)} %get-tuple-element.203) | copy-start | bytes 49156
  213.8 169.6 %copy-start = (f32[4096]{0:T(1024)S(1)}, f32[4096]{0:T(1024)}, u32[]{:S(2)}) copy-start(f32[4096]{0:T(1024)} %get-tuple-element.204) | copy-start | bytes 49156
  616.1 78.8 %copy-start.5 = (f32[4096]{0:T(1024)S(1)}, f32[4096]{0:T(1024)}, u32[]{:S(2)}) copy-start(f32[4096]{0:T(1024)} %get-tuple-element.198) | copy-start | bytes 49156
  649.2 126.6 %copy-start.3 = (f32[4096]{0:T(1024)S(1)}, f32[4096]{0:T(1024)}, u32[]{:S(2)}) copy-start(f32[4096]{0:T(1024)} %get-tuple-element.199) | copy-start | bytes 49156
  728.0 129.2 %copy-start.1 = (f32[4096]{0:T(1024)S(1)}, f32[4096]{0:T(1024)}, u32[]{:S(2)}) copy-start(f32[4096]{0:T(1024)} %get-tuple-element.200) | copy-start | bytes 49156
Sparse Core Ops, SparseCore 0:
  39.7 72.8 all-reduce.10
  545.7 70.3 all-reduce.8
